TPU v7x, 512 devices: a whole 4x4x16 slice. The times are simulated.
512 devices in a mesh: dp: 32 (over y, z_lo), mp: 16 (over x, z_hi, core).
Axes of the slice: x: 4, y: 4, z: 16 (z_hi: 2, z_lo: 8; z = z_hi * 8 + z_lo), core: 2. Of those that a mesh axis runs over, the one named last changes fastest.
Arguments:
- logits: bfloat16 [4096, 65536], P('dp', 'mp'), may hold values from -72 to 240
- targets: int32 [4096], P('dp'), may hold values from 0 to 65535
- resp_mask: int32 [4096], P('dp'), may hold values from 0 to 1, as said below
- rewards: int32 [32], P('dp'), may hold values from 0 to 10
- groups: int32 [32], P('dp'), may hold values from 0 to 7, as said below
- unit_grad: bfloat16 [4096, 8192], P(('dp', 'mp')), may hold values from -192 to 192
- mix: bfloat16 [4096, 8192], P('dp', 'mp'), may hold values from -6 to 6
- w_out: bfloat16 [8192, 8192], P('mp', 'dp'), may hold values from -0.0625 to 0.0625
Outputs:
- token_logprob: float32 [4096], P('dp')
- policy_loss: float32 [], replicated
- grad_mix: bfloat16 [4096, 8192], P('dp', 'mp')
- grad_w_out: bfloat16 [8192, 8192], P('mp', 'dp')
Inputs may be any that keep to these rules, and one draw needn't show every extreme that they name: `resp_mask`: in each sample the response mask is a run of ones followed by zeros, with at least 32 ones. `groups`: each prompt id names exactly 4 samples.
All inputs are finite; a program needn't handle non-finite values.
Results may differ from a plain program's by a relative error of at most 0.005.
Values may be sent and summed in bfloat16 or wider, within the bound.
A program may use at most 64 MiB of HBM per device.

v0:
```python
import jax
import jax.numpy as jnp
from jax import lax
from jax.sharding import Mesh
from jax.sharding import PartitionSpec as P

K = 4
DP = ("dp_0", "dp_1")
DP_MP = ("dp_0", "dp_1", "mp")


def from_everyone(shard, axis):
    count = lax.axis_size(axis)
    return lax.all_to_all(
        jnp.broadcast_to(shard[None], (count, *shard.shape)), axis, 0, 0, tiled=True
    )


def collected_together(shard, axis):
    leaves = jax.tree.leaves(shard)
    sequence = sorted(range(len(leaves)), key=lambda k: -leaves[k].size)
    width = (1, *leaves[sequence[0]].shape)[-1]
    lines = [
        jnp.pad(leaves[k].reshape(-1), (0, -leaves[k].size % width)).reshape(-1, width)
        for k in sequence
    ]
    both, at, found = (from_everyone(jnp.concatenate(lines), axis), 0, {})
    for k, line in zip(sequence, lines):
        piece = both[:, at : at + len(line)].reshape(len(both), -1)
        found[k] = piece[:, : leaves[k].size].reshape(-1, *leaves[k].shape)
        at += len(line)
    numbers = iter(range(len(leaves)))
    return jax.tree.map(lambda _: found[next(numbers)], shard)


def joined_by_halves(pieces, combine):
    while len(jax.tree.leaves(pieces)[0]) > 1:
        pieces = jax.vmap(combine)(
            *(jax.tree.map(lambda part: part[side::2], pieces) for side in (0, 1))
        )
    return jax.tree.map(lambda part: part[0], pieces)


def merged(shard, axis, combine):
    pieces = collected_together(shard, axis)
    return joined_by_halves(pieces, combine)


def of_everyone(shard, axis):
    everything = from_everyone(shard, axis)
    return jnp.sum(everything, axis=0)


def packed_total(arrays, axis):
    vector, at, gathered = (jnp.concatenate([a.reshape(-1) for a in arrays]), 0, [])
    total = of_everyone(vector, axis)
    for a in arrays:
        gathered.append(total[at : at + a.size].reshape(a.shape))
        at += a.size
    return tuple(gathered)


def whole_of(shard, axes, dim):
    for axis in reversed(axes):
        shard = lax.all_gather(shard, axis, axis=dim, tiled=True)
    return shard


def merge_stats(first, second):
    highest = jnp.maximum(first[0], second[0])
    summed = first[1] * jnp.exp(first[0] - highest) + second[1] * jnp.exp(second[0] - highest)
    return (highest, summed, first[2] + second[2])


def shards(logits, targets, resp_mask, rewards, groups, unit_grad, mix, w_out):
    tok_rows, vocab_dev = logits.shape
    mp_lane = lax.axis_index("mp")
    local_target = targets - mp_lane * vocab_dev
    present = (local_target >= 0) & (local_target < vocab_dev)
    picked = jnp.take_along_axis(logits, jnp.clip(local_target, 0, vocab_dev - 1)[:, None], axis=1)[
        :, 0
    ]
    picked = jnp.where(present, picked.astype(jnp.float32), 0.0)
    local_max = jnp.max(logits, axis=1).astype(jnp.float32)
    local_sum = jnp.sum(jnp.exp(logits.astype(jnp.float32) - local_max[:, None]), axis=1)
    highest, summed, target_logit = merged((local_max, local_sum, picked), "mp", merge_stats)
    logprob = target_logit - (highest + jnp.log(summed))
    mask_float = resp_mask.astype(jnp.float32)
    local_count = jnp.sum(mask_float)
    reward_float = rewards.astype(jnp.float32)
    prompt_slots = jnp.arange(lax.axis_size(DP) // K, dtype=jnp.int32)
    own_slot = (prompt_slots == groups[0]).astype(jnp.float32)
    group_total, token_count = packed_total((own_slot * reward_float[0], local_count), DP)
    own_total = jnp.sum(own_slot * group_total)
    advantage = reward_float[0] - (own_total - reward_float[0]) / (K - 1)
    weight = advantage * mask_float / token_count
    policy_loss = of_everyone(-jnp.sum(weight * logprob), DP)
    sub_rows = unit_grad.shape[0]
    part_weight = lax.dynamic_slice_in_dim(weight, mp_lane * sub_rows, sub_rows)
    grad_local = (-part_weight[:, None] * unit_grad.astype(jnp.float32)).astype(jnp.bfloat16)
    grad_group = lax.all_gather(grad_local, "mp", axis=0, tiled=True)
    grad_mix = lax.dot_general(
        grad_group,
        whole_of(w_out, DP, 1),
        (((1,), (1,)), ((), ())),
        preferred_element_type=jnp.float32,
    ).astype(jnp.bfloat16)
    grad_every = lax.all_to_all(grad_group, DP, split_axis=1, concat_axis=0, tiled=True)
    grad_w_out = lax.dot_general(
        lax.all_gather(mix, DP, axis=0, tiled=True),
        grad_every,
        (((0,), (0,)), ((), ())),
        preferred_element_type=jnp.float32,
    ).astype(jnp.bfloat16)
    return (logprob, policy_loss, grad_mix, grad_w_out)


def solution(mesh):
    finer = Mesh(mesh.devices.reshape(4, 8, mesh.shape["mp"]), ("dp_0", "dp_1", "mp"))
    in_specs = (P(DP, "mp"), P(DP), P(DP), P(DP), P(DP), P(DP_MP, None), P(DP, "mp"), P("mp", DP))
    out_specs = (P(DP), P(), P(DP, "mp"), P("mp", DP))
    return jax.shard_map(
        shards, mesh=finer, in_specs=in_specs, out_specs=out_specs, check_vma=False
    )
```

profile of v0, /device:TPU:1, one launch (start us, length us, event | category | flops | bytes accessed | tf_op | source)
XLA Modules:
  0.0 562.9 jit_solution(692002191340332963)
XLA Ops:
  7.2 1.3 convert_reduce_fusion
  9.8 0.7 pad_maximum_fusion.1
  11.2 16.1 %all-to-all-start.1 = ((f32[32,1,9]{2,1,0:T(1,128)}), f32[32,1,9]{2,1,0:T(1,128)S(1)}, u32[]{:S(2)}, u32[]{:S(2)}) async-start(f32[32,1,9]{2,1,0:T(1,128)} %broadcast_in_dim.17), calls=%async_computation.1 | async-start | bytes 32768 | tf_op jit(solution)/shard_map/all_to_all | solution.py:14
  27.3 0.7 all-gather.7.cloned.1.call-update
  28.7 2.3 gather_fusion
  31.0 1.4 reduce_max.9
  32.5 1.7 exponential_reduce_fusion
  34.2 4.3 all-to-all-done.1
  39.2 12.2 %all-to-all-start = ((f32[16,3,128]{2,1,0:T(4,128)}), f32[16,3,128]{2,1,0:T(4,128)S(1)}, u32[]{:S(2)}, u32[]{:S(2)}) async-start(f32[16,3,128]{2,1,0:T(4,128)} %broadcast_in_dim.16), calls=%async_computation | async-start | bytes 65536 | tf_op jit(solution)/shard_map/all_to_all | solution.py:14
  53.3 12.7 %all-to-all-done = f32[16,3,128]{2,1,0:T(4,128)S(1)} async-done(((f32[16,3,128]{2,1,0:T(4,128)}), f32[16,3,128]{2,1,0:T(4,128)S(1)}, u32[]{:S(2)}, u32[]{:S(2)}) %all-to-all-start) | async-done | bytes 24608 | tf_op jit(solution)/shard_map/all_to_all | solution.py:14
  66.4 1.8 multiply_reduce_fusion
  68.2 0.7 multiply_convert_fusion
  69.8 30.2 %all-gather.7.cloned.1.call-done = bf16[512,2048]{1,0:T(8,128)(2,1)} async-done(((bf16[512,256]{1,0:T(8,128)(2,1)}), bf16[512,2048]{1,0:T(8,128)(2,1)}) %all-gather.7.cloned.1.call-update) | async-done | bytes 2097168 | tf_op jit(solution)/shard_map/all_gather | solution.py:65
  101.3 9.4 %all-to-all-start.2 = ((f32[32,1,1]{2,1,0:T(1,128)}), f32[32,1,1]{2,1,0:T(1,128)S(1)}, u32[]{:S(2)}, u32[]{:S(2)}) async-start(f32[32,1,1]{2,1,0:T(1,128)} %broadcast_in_dim.18), calls=%async_computation.2 | async-start | bytes 32768 | tf_op jit(solution)/shard_map/all_to_all | solution.py:14
  110.6 83.5 %all-gather.5.cloned.1.call-done = bf16[128,8192]{1,0:T(8,128)(2,1)} async-done(((bf16[8,8192]{1,0:T(8,128)(2,1)}), bf16[128,8192]{1,0:T(8,128)(2,1)}) %all-gather.5.cloned.1.call-update) | async-done | bytes 2097168 | tf_op jit(solution)/shard_map/all_gather | solution.py:101
  194.1 4.1 copy.39
  198.2 4.8 all-to-all-start.3
  203.7 125.4 %all-to-all-done.3 = bf16[128,32,256]{0,2,1:T(8,128)(2,1)S(1)} async-done(((bf16[128,32,256]{0,2,1:T(8,128)(2,1)}), bf16[128,32,256]{0,2,1:T(8,128)(2,1)S(1)}, u32[]{:S(2)}, u32[]{:S(2)}) %all-to-all-start.3) | async-done | bytes 2097184 | tf_op jit(solution)/shard_map/all_to_all | solution.py:108
  329.1 2.9 copy.40
  332.0 111.9 %all-gather.11.cloned.1.call-done = bf16[4096,512]{1,0:T(8,128)(2,1)} async-done(((bf16[128,512]{1,0:T(8,128)(2,1)}), bf16[4096,512]{1,0:T(8,128)(2,1)}) %all-gather.11.cloned.1.call-update) | async-done | bytes 4194320 | tf_op jit(solution)/shard_map/all_gather | solution.py:110
  443.9 4.2 fusion
  448.2 0.8 copy.41
  449.0 100.4 %all-gather.9.cloned.1.call-done = bf16[512,8192]{1,0:T(8,128)(2,1)} async-done(((bf16[512,2048]{1,0:T(8,128)(2,1)}), bf16[512,8192]{1,0:T(8,128)(2,1)}) %all-gather.9.cloned.1.call-update) | async-done | bytes 8388624 | tf_op jit(solution)/shard_map/all_gather | solution.py:65
  549.4 7.0 %convolution_convert_fusion.1 = bf16[128,512]{1,0:T(8,128)(2,1)} fusion(bf16[128,8192]{1,0:T(8,128)(2,1)S(1)} %copy-done, bf16[512,8192]{1,0:T(8,128)(2,1)} %all-gather.9.cloned.1.call-done), kind=kOutput, calls=%fused_computation.4 | convolution fusion | flops 1073807360 | bytes 10616832 | tf_op jit(solution)/shard_map/dot_general | solution.py:102
  (57 shorter events, 5.9 us)
Async XLA Ops:
  7.2 59.2 %copy-start.2 = (s32[128]{0:T(128)S(1)}, s32[128]{0:T(128)}, u32[]{:S(2)}) copy-start(s32[128]{0:T(128)} %param.10) | copy-start | bytes 1540
  7.2 27.0 %copy-start.3 = (s32[128]{0:T(128)S(1)}, s32[128]{0:T(128)}, u32[]{:S(2)}) copy-start(s32[128]{0:T(128)} %param.9) | copy-start | bytes 1540
  7.2 61.1 %copy-start.1 = (bf16[8,8192]{1,0:T(8,128)(2,1)S(1)}, bf16[8,8192]{1,0:T(8,128)(2,1)}, u32[]{:S(2)}) copy-start(bf16[8,8192]{1,0:T(8,128)(2,1)} %param.13) | copy-start | bytes 393220
  11.2 27.4 %all-to-all-start.1 = ((f32[32,1,9]{2,1,0:T(1,128)}), f32[32,1,9]{2,1,0:T(1,128)S(1)}, u32[]{:S(2)}, u32[]{:S(2)}) async-start(f32[32,1,9]{2,1,0:T(1,128)} %broadcast_in_dim.17), calls=%async_computation.1 | async-start | bytes 32768 | tf_op jit(solution)/shard_map/all_to_all | solution.py:14
  27.2 72.7 %all-gather.7.cloned.1.call-start = ((), (), s32[]{:S(2)}) async-start(), calls=%async_computation.5 | async-start | bytes 2359296 | tf_op jit(solution)/shard_map/all_gather | solution.py:65
  39.2 26.8 %all-to-all-start = ((f32[16,3,128]{2,1,0:T(4,128)}), f32[16,3,128]{2,1,0:T(4,128)S(1)}, u32[]{:S(2)}, u32[]{:S(2)}) async-start(f32[16,3,128]{2,1,0:T(4,128)} %broadcast_in_dim.16), calls=%async_computation | async-start | bytes 65536 | tf_op jit(solution)/shard_map/all_to_all | solution.py:14
  51.3 142.8 %all-gather.5.cloned.1.call-start = ((), (), s32[]{:S(2)}) async-start(), calls=%async_computation.4 | async-start | bytes 2228224 | tf_op jit(solution)/shard_map/all_gather | solution.py:101
  69.0 374.9 %all-gather.11.cloned.1.call-start = ((), (), s32[]{:S(2)}) async-start(), calls=%async_computation.7 | async-start | bytes 4325376 | tf_op jit(solution)/shard_map/all_gather | solution.py:110
  69.8 479.6 %all-gather.9.cloned.1.call-start = ((), (), s32[]{:S(2)}) async-start(), calls=%async_computation.6 | async-start | bytes 10485760 | tf_op jit(solution)/shard_map/all_gather | solution.py:65
  101.3 96.9 %all-to-all-start.2 = ((f32[32,1,1]{2,1,0:T(1,128)}), f32[32,1,1]{2,1,0:T(1,128)S(1)}, u32[]{:S(2)}, u32[]{:S(2)}) async-start(f32[32,1,1]{2,1,0:T(1,128)} %broadcast_in_dim.18), calls=%async_computation.2 | async-start | bytes 32768 | tf_op jit(solution)/shard_map/all_to_all | solution.py:14
  198.2 130.9 %all-to-all-start.3 = ((bf16[128,32,256]{0,2,1:T(8,128)(2,1)}), bf16[128,32,256]{0,2,1:T(8,128)(2,1)S(1)}, u32[]{:S(2)}, u32[]{:S(2)}) async-start(bf16[128,32,256]{0,2,1:T(8,128)(2,1)} %bitcast.14), calls=%async_computation.3 | async-start | bytes 4194304 | tf_op jit(solution)/shard_map/all_to_all | solution.py:108
  443.9 105.5 %copy-start = (bf16[128,8192]{1,0:T(8,128)(2,1)S(1)}, bf16[128,8192]{1,0:T(8,128)(2,1)}, u32[]{:S(2)}) copy-start(bf16[128,8192]{1,0:T(8,128)(2,1)} %all-gather.5.cloned.1.call-done) | copy-start | bytes 6291460
Sparse Core Ops, SparseCore 0:
  30.1 69.8 all-gather.6
  103.8 90.2 all-gather.4
  196.2 247.6 all-gather.10
  445.9 103.4 all-gather.8
where the time goes:
time: 564 us; the launch traced here: 563 us
  waiting for transfers between devices  470 us (83%)
  starting transfers between devices  42.6 us (8%)
  between operations  16.5 us (3%)
  local copies, waits for them, and re-layouts  12.9 us (2%)
  matrix products  11.2 us (2%)
  other arithmetic  9.9 us (2%)
    all_gather x2, waiting for transfers between devices, whole_of(): shard = lax.all_gather(shard, axis, axis=dim, tiled=True)  131 us
    all_to_all x1, waiting for transfers between devices, shards(): lax.all_to_all(grad_group, DP, split_axis=1, concat_axis=0, tiled=True)  125 us
    all_gather x1, waiting for transfers between devices, shards(): lax.all_gather(mix, DP, axis=0, tiled=True)  112 us
    all_gather x1, waiting for transfers between devices, shards(): grad_group = lax.all_gather(grad_local, 'mp', axis=0, tiled=True)  83.5 us
    all_to_all x3, starting transfers between devices, from_everyone(): lax.all_to_all(jnp.broadcast_to(shard[None], (count, *shard.shape)), axis...  37.6 us
    all_to_all x3, waiting for transfers between devices, from_everyone(): lax.all_to_all(jnp.broadcast_to(shard[None], (count, *shard.shape)), axis...  17 us
  transfers between devices with their start and end apart: 8, of which 7 were waited for; matrix products, arithmetic and copies ran while one was open for 4% of the time, Pallas kernels for 0%

commit v1 on v0

v1 whole, which is shorter than its diff:
```python
import jax
import jax.numpy as jnp
from jax import lax
from jax.sharding import Mesh
from jax.sharding import PartitionSpec as P

K = 4
Y, Z = "dp_0", "dp_1"
DP = (Y, Z)
DP_MP = (Y, Z, "mp")


def shards(logits, targets, resp_mask, rewards, groups, unit_grad, mix, w_out):
    rows, vocab = logits.shape
    lane = lax.axis_index("mp")
    ny, nz, nmp = lax.axis_size(Y), lax.axis_size(Z), lax.axis_size("mp")
    wide = logits.astype(jnp.float32)
    local_target = targets - lane * vocab
    hit = lax.broadcasted_iota(jnp.int32, logits.shape, 1) == local_target[:, None]
    picked = jnp.sum(jnp.where(hit, wide, 0.0), axis=1)
    local_max = jnp.max(wide, axis=1)
    local_sum = jnp.sum(jnp.exp(wide - local_max[:, None]), axis=1)
    stats = lax.all_gather(jnp.stack([local_max, local_sum, picked]), "mp")
    top = jnp.max(stats[:, 0], axis=0)
    total = jnp.sum(stats[:, 1] * jnp.exp(stats[:, 0] - top), axis=0)
    logprob = jnp.sum(stats[:, 2], axis=0) - (top + jnp.log(total))

    length = jnp.sum(resp_mask)
    info = jnp.stack([rewards[0], groups[0], length]).astype(jnp.float32)
    every = lax.all_gather(info, DP)
    reward, group, count = every[:, 0], every[:, 1], every[:, 2]
    same = (group[:, None] == group[None, :]).astype(jnp.float32)
    own_total = jnp.sum(same * reward[None, :], axis=1)
    scale = (reward - (own_total - reward) / (K - 1)) / jnp.sum(count)
    token_count = jnp.sum(count)
    advantage = reward - (own_total - reward) / (K - 1)
    me = lax.axis_index(Y) * nz + lax.axis_index(Z)
    mask = resp_mask.astype(jnp.float32)
    weight = advantage[me] * mask / token_count
    policy_loss = jnp.sum(lax.all_gather(-jnp.sum(weight * logprob), DP))

    sub = unit_grad.shape[0]
    part = lax.dynamic_slice_in_dim(weight, lane * sub, sub)
    grad = (-part[:, None] * unit_grad.astype(jnp.float32)).astype(jnp.bfloat16)
    depth = w_out.shape[1]
    grad = grad.reshape(sub, ny, nz, depth).transpose(2, 0, 1, 3).reshape(nz, sub, ny * depth)
    grad = lax.all_to_all(grad, Z, 0, 0, tiled=True)
    grad = lax.all_gather(grad, "mp", axis=1, tiled=True).reshape(nz * rows, ny * depth)
    w_cols = lax.all_gather(w_out, Y, axis=1, tiled=True)
    mix_rows = lax.all_gather(mix, Z, axis=0, tiled=True)
    part_mix = lax.dot_general(
        grad, w_cols, (((1,), (1,)), ((), ())), preferred_element_type=jnp.float32
    ).astype(jnp.bfloat16)
    grad_mix = lax.psum_scatter(part_mix, Z, scatter_dimension=0, tiled=True)
    part_w = lax.dot_general(
        mix_rows, grad, (((0,), (0,)), ((), ())), preferred_element_type=jnp.float32
    ).astype(jnp.bfloat16)
    grad_w_out = lax.psum_scatter(part_w, Y, scatter_dimension=1, tiled=True)
    return logprob, policy_loss, grad_mix, grad_w_out


def solution(mesh):
    finer = Mesh(mesh.devices.reshape(4, 8, mesh.shape["mp"]), ("dp_0", "dp_1", "mp"))
    in_specs = (P(DP, "mp"), P(DP), P(DP), P(DP), P(DP), P(DP_MP, None), P(DP, "mp"), P("mp", DP))
    out_specs = (P(DP), P(), P(DP, "mp"), P("mp", DP))
    return jax.shard_map(
        shards, mesh=finer, in_specs=in_specs, out_specs=out_specs, check_vma=False
    )
```

time: 564 us -> 449 us (0.80)
  the two profiles are of different devices: /device:TPU:1 before, /device:TPU:4 now
where the time goes in v1:
time: 449 us
  blocking collectives  303 us (67%)
  waiting for transfers between devices  107 us (24%)
  between operations  15.8 us (4%)
  other arithmetic  10.2 us (2%)
  matrix products  7.8 us (2%)
  local copies, waits for them, and re-layouts  4.67 us (1%)
    all_gather x1, blocking collectives, shards(): every = lax.all_gather(info, DP)  125 us
    unnamed x1, blocking collectives  124 us
    all_gather x1, waiting for transfers between devices, shards(): lax.all_gather(grad, 'mp', axis=1, tiled=True)  82.7 us
    all_gather x1, blocking collectives, shards(): stats = lax.all_gather(jnp.stack([local_max, local_sum, picked]), 'mp')  37.7 us
    all_gather x1, waiting for transfers between devices, shards(): w_cols = lax.all_gather(w_out, Y, axis=1, tiled=True)  23.2 us
    all_to_all x1, blocking collectives, shards(): grad = lax.all_to_all(grad, Z, 0, 0, tiled=True)  15.8 us
  transfers between devices with their start and end apart: 5, of which 2 were waited for; matrix products, arithmetic and copies ran while one was open for 5% of the time, Pallas kernels for 0%

profile of v1, /device:TPU:4, one launch (start us, length us, event | category | flops | bytes accessed | tf_op | source)
XLA Modules:
  0.0 448.6 jit_solution(11722143457326987204)
XLA Ops:
  7.2 0.7 all-gather.11.cloned.1.call-update
  9.3 1.3 reduce_sum.85
  10.6 0.7 fusion.4
  11.3 125.1 %all-gather.2 = f32[32,1,3]{2,1,0:T(1,128)S(1)} all-gather(f32[1,1,3]{2,1,0:T(1,128)S(1)} %fusion.4), channel_id=1, replica_groups=mesh['dp_0'=4,'dp_1'=8,'mp'=16] {'dp_0','dp_1'}, dimensions={0}, use_global_device_ids=true | all-gather | bytes 396 | tf_op jit(solution)/shard_map/all_gather | solution.py:30
  136.4 0.6 slice_bitcast_fusion
  137.0 0.2 select_reduce_fusion
  137.2 1.4 reduce_max.27
  138.7 0.7 broadcast_subtract_fusion
  139.3 2.0 fusion.1
  141.4 37.7 %all-gather.1 = f32[16,3,128]{2,1,0:T(4,128)S(1)} all-gather(f32[1,3,128]{2,1,0:T(4,128)S(1)} %maximum_bitcast_fusion), channel_id=2, replica_groups=mesh['dp_0'=4,'dp_1'=8,'mp'=16] {'mp'}, dimensions={0}, use_global_device_ids=true | all-gather | bytes 26112 | tf_op jit(solution)/shard_map/all_gather | solution.py:23
  179.1 0.6 dynamic_slice.6
  179.7 2.4 multiply_reduce_fusion.1
  182.3 0.1 copy.29
  182.5 15.8 %all_to_all.5 = bf16[8,8,1024]{2,1,0:T(8,128)(2,1)} all-to-all(bf16[8,8,1024]{2,1,0:T(8,128)(2,1)S(1)} %reshape.79), channel_id=1, replica_groups=mesh['dp_0'=4,'dp_1'=8,'mp'=16] {'dp_1'}, dimensions={0} | all-to-all | bytes 262144 | tf_op jit(solution)/shard_map/all_to_all | solution.py:47
  198.3 0.7 all-gather.9.cloned.1.call-update
  199.1 82.7 %all-gather.7.cloned.1.call-done = bf16[8,128,1024]{2,1,0:T(8,128)(2,1)} async-done(((bf16[8,8,1024]{2,1,0:T(8,128)(2,1)}), bf16[8,128,1024]{2,1,0:T(8,128)(2,1)}) %all-gather.7.cloned.1.call-update) | async-done | bytes 2097168 | tf_op jit(solution)/shard_map/all_gather | solution.py:48
  281.8 4.3 fusion.3
  286.1 23.2 %all-gather.9.cloned.1.call-done = bf16[512,1024]{1,0:T(8,128)(2,1)} async-done(((bf16[512,256]{1,0:T(8,128)(2,1)}), bf16[512,1024]{1,0:T(8,128)(2,1)}) %all-gather.9.cloned.1.call-update) | async-done | bytes 1048592 | tf_op jit(solution)/shard_map/all_gather | solution.py:49
  309.4 3.5 convolution_convert_fusion.1
  313.6 1.3 dynamic-slice
  314.8 0.8 dynamic-update-slice
  315.6 124.1 %all-reduce = f32[32]{0:T(128)S(1)} all-reduce(f32[32]{0:T(128)S(1)} %dynamic-update-slice), channel_id=1, replica_groups=mesh['dp_0'=4,'dp_1'=8,'mp'=16] {'dp_0','dp_1'}, use_global_device_ids=true, to_apply=%add | all-reduce | flops 32 | bytes 256
  439.7 0.6 reduce_sum.89
  440.3 1.8 copy.26
  (27 shorter events, 0.7 us)
Async XLA Ops:
  7.2 172.5 %copy-start.1 = (s32[128]{0:T(128)S(1)}, s32[128]{0:T(128)}, u32[]{:S(2)}) copy-start(s32[128]{0:T(128)} %param.10) | copy-start | bytes 1540
  7.2 175.0 %copy-start = (bf16[8,8192]{1,0:T(8,128)(2,1)S(1)}, bf16[8,8192]{1,0:T(8,128)(2,1)}, u32[]{:S(2)}) copy-start(bf16[8,8192]{1,0:T(8,128)(2,1)} %param.13) | copy-start | bytes 393220
  7.2 191.9 %all-gather.11.cloned.1.call-start = ((), (), s32[]{:S(2)}) async-start(), calls=%async_computation.6 | async-start | bytes 1179648 | tf_op jit(solution)/shard_map/all_gather | solution.py:50
  7.9 273.9 %all-gather.7.cloned.1.call-start = ((), (), s32[]{:S(2)}) async-start(), calls=%async_computation.3 | async-start | bytes 2228224 | tf_op jit(solution)/shard_map/all_gather | solution.py:48
  198.3 111.1 %all-gather.9.cloned.1.call-start = ((), (), s32[]{:S(2)}) async-start(), calls=%async_computation.4 | async-start | bytes 1310720 | tf_op jit(solution)/shard_map/all_gather | solution.py:49
  199.0 241.3 %reduce-scatter.5.cloned.1.call-start = ((), (), s32[]{:S(2)}) async-start(), calls=%async_computation.7 | async-start | bytes 1310720 | tf_op jit(solution)/shard_map/reduce_scatter | solution.py:58
  281.8 27.6 %copy-start.2 = (bf16[8,128,1024]{2,1,0:T(8,128)(2,1)S(1)}, bf16[8,128,1024]{2,1,0:T(8,128)(2,1)}, u32[]{:S(2)}) copy-start(bf16[8,128,1024]{2,1,0:T(8,128)(2,1)} %all-gather.7.cloned.1.call-done) | copy-start | bytes 6291460
  286.1 156.0 %reduce-scatter.3.cloned.1.call-start = ((), (), s32[]{:S(2)}) async-start(), calls=%async_computation.5 | async-start | bytes 1179648 | tf_op jit(solution)/shard_map/reduce_scatter | solution.py:54
Sparse Core Ops, SparseCore 0:
  10.1 71.0 all-gather.10
  198.4 83.3 all-gather.6
  283.9 25.4 all-gather.8
  312.0 32.5 reduce-scatter.4
  347.8 67.9 reduce-scatter.2

commit v2 on v1

v2 whole, which is shorter than its diff:
```python
import jax
import jax.numpy as jnp
from jax import lax
from jax.experimental import pallas as pl
from jax.experimental.pallas import tpu as pltpu
from jax.sharding import Mesh
from jax.sharding import PartitionSpec as P

K = 4
NY, NZ, NX = 4, 8, 4
DP = ("y", "zl")
MP = ("x", "zh", "core")
F32, BF16 = jnp.float32, jnp.bfloat16
NT = (((1,), (1,)), ((), ()))
TN = (((0,), (0,)), ((), ()))
SUB = 4


def kernel(
    logits, targets, mask, rewards, groups, ug, mix, w_out,
    lp_out, loss_out, gmix_out, gw_out,
    LG, US, GR, MX, W, G2, PF, RB, SB, GW, YS, YR, INFO, WSC, LSC, STA, STB, LZ, LY,
    lsem, zsem, xsem, dsem, msem, wsem, rsem, ysem, ssem, mssem, sends,
):
    y, k, x = lax.axis_index("y"), lax.axis_index("zl"), lax.axis_index("x")
    h, c = lax.axis_index("zh"), lax.axis_index("core")
    rows, vocab = LG.shape
    depth = W.shape[2]
    xr, xl = lax.rem(x + 1, NX), lax.rem(x + NX - 1, NX)
    xo = lax.rem(x + 2, NX)
    yr, yl = lax.rem(y + 1, NY), lax.rem(y + NY - 1, NY)
    yo = lax.rem(y + 2, NY)
    right, left, opp = {"zl": k + 1}, {"zl": k - 1}, {"core": 1 - c}

    def idx(xx, cc, zz, hh):
        return ((xx * 2 + cc) * NZ + zz) * 2 + hh

    def unit(xx, cc, zz):
        return GR.at[pl.ds(idx(xx, cc, zz, 0), 2)]

    def put(src, dst, send, recv, where):
        pltpu.make_async_remote_copy(
            src_ref=src, dst_ref=dst, send_sem=send, recv_sem=recv,
            device_id=where, device_id_type=pl.DeviceIdType.MESH,
        ).start()

    def take(ref, sem):
        pltpu.make_async_copy(ref, ref, sem).wait()

    def cols(i):
        return pl.ds(pl.multiple_of(i * depth, depth), depth)

    load_logits = pltpu.make_async_copy(logits, LG, lsem.at[0])
    load_logits.start()
    for yy in range(NY):
        for zz in range(NZ):
            pltpu.make_async_copy(
                ug.at[:, pl.ds((yy * NZ + zz) * depth, depth)],
                US.at[zz, :, pl.ds(yy * depth, depth)], lsem.at[1],
            ).start()
    for yy in range(NY):
        pltpu.make_async_copy(
            ug.at[:, cols(yy * NZ + k)],
            GR.at[idx(x, c, k, h), :, pl.ds(yy * depth, depth)], zsem.at[k],
        ).start()
    own_rows = pl.ds(pl.multiple_of(k * rows, rows), rows)
    for q in range(SUB):
        pltpu.make_async_copy(
            mix.at[:, pl.ds(q * 128, 128)], MX.at[q, own_rows], lsem.at[2]
        ).start()
    load_w = pltpu.make_async_copy(w_out, W.at[y], lsem.at[3])
    load_w.start()

    barrier = pltpu.get_barrier_semaphore()
    peers = []
    for step in range(1, 2 * NZ):
        place = lax.rem(h * NZ + k + step, 2 * NZ)
        peers.append({"zh": place // NZ, "zl": lax.rem(place, NZ)})
    peers += [{"y": lax.rem(y + i, NY)} for i in range(1, NY)]
    peers += [{"x": lax.rem(x + i, NX)} for i in range(1, NX)]
    peers += [opp, {"zh": 1 - h, "core": 1 - c}]
    for peer in peers:
        pl.semaphore_signal(barrier, inc=1, device_id=peer, device_id_type=pl.DeviceIdType.MESH)

    lane = lax.broadcasted_iota(jnp.int32, (1, 128), 1)
    length = jnp.sum(mask[...].astype(F32), axis=1, keepdims=True)
    facts = jnp.where(lane == 0, rewards[0].astype(F32), 0.0)
    facts = facts + jnp.where(lane == 1, groups[0].astype(F32), 0.0)
    facts = facts + jnp.where(lane == 2, jnp.broadcast_to(length, (1, 128)), 0.0)
    INFO[y * NZ + k] = facts

    load_logits.wait()
    eye = lax.broadcasted_iota(jnp.int32, (rows, rows), 0) == lax.broadcasted_iota(
        jnp.int32, (rows, rows), 1
    )
    column = lax.broadcasted_iota(jnp.int32, (rows, 128), 1).astype(F32)
    shift = ((x * 2 + h) * 2 + c) * vocab
    wanted = (targets[...] - shift).astype(F32)
    wanted = jnp.sum(jnp.where(eye, wanted, 0.0), axis=1, keepdims=True)

    def piece(j):
        return LG[:, pl.ds(pl.multiple_of(j * 128, 128), 128)].astype(F32)

    tiles = vocab // 128
    peak = lax.fori_loop(
        0, tiles, lambda j, m: jnp.maximum(m, piece(j)), jnp.full((rows, 128), -jnp.inf, F32)
    )
    peak = jnp.max(peak, axis=1, keepdims=True)

    def collect(j, carry):
        total, found = carry
        value = piece(j)
        total = total + jnp.exp(value - peak)
        at = wanted - (j * 128).astype(F32)
        return total, found + jnp.where(column == at, value, 0.0)

    zero = jnp.zeros((rows, 128), F32)
    total, found = lax.fori_loop(0, tiles, collect, (zero, zero))

    def as_row(v):
        return jnp.sum(jnp.where(eye, v, 0.0), axis=0, keepdims=True)

    a = h * 2 + c
    STA[a, 0:1, :] = as_row(peak)
    STA[a, 1:2, :] = as_row(jnp.sum(total, axis=1, keepdims=True))
    STA[a, 2:3, :] = as_row(jnp.sum(found, axis=1, keepdims=True))

    for ref, sem in ((US, lsem.at[1]), (MX.at[:, own_rows], lsem.at[2])):
        take(ref, sem)
    load_w.wait()
    pl.semaphore_wait(barrier, len(peers))

    me = y * NZ + k
    for i in range(1, NZ):
        to = lax.rem(k + i, NZ)
        put(INFO.at[me], INFO.at[me], sends.at[0], ssem.at[0], {"zl": to})
    mine = idx(x, c, k, h)
    for far in range(NZ - 1, -1, -1):
        for side in (1, -1) if far else (1,):
            to = k + side * far

            def send_rows(to=to, far=far):
                for hh in (0, 1):
                    if far == 0 and hh == 0:
                        continue
                    zh = hh if far else 1 - h
                    put(US.at[to], GR.at[mine], sends.at[1], zsem.at[k], {"zl": to, "zh": zh})

            if far == 0:
                send_rows()
            else:
                pl.when((to >= 0) & (to < NZ))(send_rows)
    half = W.shape[1] // 2
    first, second = pl.ds(0, half), pl.ds(half, half)
    put(W.at[y, first], W.at[y, first], sends.at[2], wsem.at[0], {"y": yr})
    put(W.at[y, second], W.at[y, second], sends.at[2], wsem.at[3], {"y": yl})
    put(W.at[y, second], W.at[y, second], sends.at[2], wsem.at[1], {"y": yr})
    put(W.at[y, first], W.at[y, first], sends.at[2], wsem.at[4], {"y": yl})

    def mix_at(zz, q):
        return MX.at[q, pl.ds(pl.multiple_of(zz * rows, rows), rows)]

    def mix_hop(hop, waiting):
        def one(q, carry):
            for side, away, ok in ((0, -1, k < NZ - 1), (1, 1, k > 0)):
                origin = k + away * hop

                def forward(side=side, origin=origin, ok=ok):
                    if waiting:
                        take(mix_at(origin, q), msem.at[origin, q])

                    @pl.when(ok)
                    def _():
                        put(
                            mix_at(origin, q), mix_at(origin, q), mssem.at[side, hop],
                            msem.at[origin, q], (right, left)[side],
                        )

                pl.when((origin >= 0) & (origin < NZ))(forward)
            return carry

        lax.fori_loop(0, SUB, one, 0)

    mix_hop(0, False)
    for peer in ({"zh": 1 - h}, opp, {"zh": 1 - h, "core": 1 - c}):
        put(STA.at[a], STA.at[a], sends.at[3], ssem.at[2], peer)

    take(INFO.at[pl.ds(0, NZ - 1)], ssem.at[0])
    line = INFO.at[pl.ds(y * NZ, NZ)]
    for i in range(1, NY):
        put(line, line, sends.at[4], ssem.at[1], {"y": lax.rem(y + i, NY)})

    take(W.at[yl, first], wsem.at[0])
    put(W.at[yl, first], W.at[yl, first], sends.at[5], wsem.at[2], {"y": yr})
    take(W.at[yr, second], wsem.at[3])
    put(W.at[yr, second], W.at[yr, second], sends.at[5], wsem.at[5], {"y": yl})

    take(INFO.at[pl.ds(0, (NY - 1) * NZ)], ssem.at[1])
    count = jnp.zeros((1, 128), F32)
    for r in range(NY * NZ):
        count = count + INFO[r]
    count = jnp.broadcast_to(count[:, 2:3], (1, 128))

    def weigh(zz, carry):
        fact = INFO[y * NZ + zz]
        reward = jnp.broadcast_to(fact[:, 0:1], (1, 128))
        group = jnp.broadcast_to(fact[:, 1:2], (1, 128))
        own = jnp.zeros((1, 128), F32)
        for r in range(NY * NZ):
            other = INFO[r]
            same = jnp.broadcast_to(other[:, 1:2], (1, 128)) == group
            own = own + jnp.where(same, jnp.broadcast_to(other[:, 0:1], (1, 128)), 0.0)
        WSC[zz] = (reward - (own - reward) / (K - 1)) / count
        LSC[zz] = jnp.broadcast_to(fact[:, 2:3], (1, 128))
        return carry

    lax.fori_loop(0, NZ, weigh, 0)

    def merge(ref, n):
        top = ref[0, 0:1, :]
        for i in range(1, n):
            top = jnp.maximum(top, ref[i, 0:1, :])
        total = jnp.zeros_like(top)
        found = jnp.zeros_like(top)
        for i in range(n):
            total = total + ref[i, 1:2, :] * jnp.exp(ref[i, 0:1, :] - top)
            found = found + ref[i, 2:3, :]
        return top, total, found

    take(STA.at[pl.ds(0, 3)], ssem.at[2])
    for i, v in enumerate(merge(STA, 4)):
        STB[x, i : i + 1, :] = v

    def arrived(zz):
        take(unit(x, c, zz), zsem.at[zz])
        here = unit(x, c, zz)
        put(here, here, sends.at[6], xsem.at[0, zz], {"x": xr})
        put(here, here, sends.at[6], xsem.at[1, zz], {"x": xl})
        put(here, here, sends.at[7], dsem.at[zz], opp)

    def passed(zz):
        for side, origin, to in ((0, xl, xr), (1, xr, xl)):
            here = unit(origin, c, zz)
            take(here, xsem.at[side, zz])
            part = GR.at[idx(origin, c, zz, side)]
            put(part, part, sends.at[6], xsem.at[2 + side, zz], {"x": to})
            put(here, here, sends.at[7], dsem.at[zz], opp)

    def closed(zz):
        for side in (0, 1):
            take(GR.at[idx(xo, c, zz, side)], xsem.at[2 + side, zz])
        here = unit(xo, c, zz)
        put(here, here, sends.at[7], dsem.at[zz], opp)

    def partial(zz):
        take(GR.at[pl.ds(0, 8)], dsem.at[zz])
        weight, limit = WSC[zz], LSC[zz]
        base = pl.multiple_of(zz * rows, rows)

        def scale(i, carry):
            xx, hh = i // 2, lax.rem(i, 2)
            pair = jnp.concatenate(
                [GR[idx(xx, cc, zz, hh)].astype(F32) for cc in (0, 1)], axis=0
            )
            place = (lax.broadcasted_iota(jnp.int32, (16, 128), 0) + i * 16).astype(F32)
            factor = jnp.where(place < limit, -weight, 0.0)
            factor = jnp.concatenate([factor] * (pair.shape[1] // 128), axis=1)
            G2[pl.ds(pl.multiple_of(base + i * 16, 16), 16), :] = (factor * pair).astype(BF16)
            return carry

        lax.fori_loop(0, rows // 16, scale, 0)
        block = G2[pl.ds(base, rows), :]
        acc = None
        for yy in range(NY):
            one = lax.dot_general(
                block[:, yy * depth : (yy + 1) * depth], W[yy], NT, preferred_element_type=F32
            )
            acc = one if acc is None else acc + one
        PF[zz] = acc

    def both(far, act):
        for side in (1, -1):
            zz = k + side * far
            ok = (zz >= 0) & (zz < NZ) & (far >= 0) & (far < NZ)
            if side == -1:
                ok = ok & (far > 0)

            pl.when(ok)(lambda zz=zz: act(zz))

    step_rows = rows // SUB

    def scatter_slot(s):
        going = ((0, NZ - 1 - (s - k), s >= k, k > 0), (1, s - (NZ - 1 - k), s >= NZ - 1 - k, k < NZ - 1))

        def one(q, carry):
            part = pl.ds(pl.multiple_of(q * step_rows, step_rows), step_rows)
            for side, to, ok, more in going:

                def store(side=side, to=to, more=more):
                    @pl.when(more)
                    def _():
                        take(RB.at[side, to, part], rsem.at[side, to, q])
                        SB[to, part, :] = (PF[to, part, :] + RB[side, to, part, :].astype(F32)).astype(BF16)

                    @pl.when(jnp.logical_not(more))
                    def _():
                        SB[to, part, :] = PF[to, part, :].astype(BF16)

                pl.when(ok)(store)
            for side, to, ok, more in going:

                def send(side=side, to=to):
                    put(
                        SB.at[to, part], RB.at[side, to, part], sends.at[8],
                        rsem.at[side, to, q], (right, left)[side],
                    )

                pl.when(ok)(send)
            return carry

        lax.fori_loop(0, SUB, one, 0)

    for i in range(1, NX):
        put(STB.at[x], STB.at[x], sends.at[9], ssem.at[3], {"x": lax.rem(x + i, NX)})

    def step(t, carry):
        pl.when(t < NZ - 1)(lambda: mix_hop(t + 1, True))
        both(NZ - 1 - t, arrived)
        both(NZ - t, passed)
        both(NZ + 1 - t, closed)

        @pl.when(t == 2)
        def _():
            take(W.at[yl, second], wsem.at[1])
            take(W.at[yr, first], wsem.at[4])
            take(W.at[yo, first], wsem.at[2])
            take(W.at[yo, second], wsem.at[5])

        both(NZ + 2 - t, partial)
        pl.when((t >= 3) & (t < NZ + 2))(lambda: scatter_slot(t - 3))
        return carry

    lax.fori_loop(0, NZ + 3, step, 0)

    take(STB.at[pl.ds(0, NX - 1)], ssem.at[3])
    top, total, found = merge(STB, NX)
    logprob = found - (top + jnp.log(total))
    lp_out[...] = logprob
    weight = jnp.where(lane.astype(F32) < LSC[k], WSC[k], 0.0)
    LZ[k] = jnp.broadcast_to(-jnp.sum(weight * logprob, axis=1, keepdims=True), (1, 128))

    def product(q):
        GW[q] = lax.dot_general(MX[q], G2[...], TN, preferred_element_type=F32)

    def stage(slot, value):
        YS[slot] = value.astype(BF16)

    product(0)
    for i in range(1, NZ):
        put(LZ.at[k], LZ.at[k], sends.at[10], ssem.at[4], {"zl": lax.rem(k + i, NZ)})
    stage(0, GW[0, :, cols(yo)])
    product(2)
    put(YS.at[0], YR.at[0], sends.at[11], ysem.at[0], {"y": yr})
    stage(6, GW[2, :, cols(yo)])
    product(1)
    put(YS.at[6], YR.at[6], sends.at[11], ysem.at[6], {"y": yl})
    stage(1, GW[1, :, cols(yo)])
    stage(10, GW[0, :, cols(yl)])
    product(3)
    put(YS.at[1], YR.at[1], sends.at[11], ysem.at[1], {"y": yr})
    put(YS.at[10], YR.at[10], sends.at[11], ysem.at[10], {"y": yl})
    stage(7, GW[3, :, cols(yo)])
    stage(4, GW[2, :, cols(yr)])
    stage(5, GW[3, :, cols(yr)])
    stage(11, GW[1, :, cols(yl)])
    put(YS.at[7], YR.at[7], sends.at[11], ysem.at[7], {"y": yl})
    put(YS.at[4], YR.at[4], sends.at[11], ysem.at[4], {"y": yr})
    put(YS.at[11], YR.at[11], sends.at[11], ysem.at[11], {"y": yl})
    put(YS.at[5], YR.at[5], sends.at[11], ysem.at[5], {"y": yr})

    acc = PF[k]
    gmix_out[...] = acc.astype(BF16)
    for side, more in ((0, k > 0), (1, k < NZ - 1)):

        @pl.when(more)
        def _(side=side):
            for q in range(SUB):
                part = pl.ds(q * step_rows, step_rows)
                take(RB.at[side, k, part], rsem.at[side, k, q])
            PF[k] = PF[k] + RB[side, k].astype(F32)

    gmix_out[...] = PF[k].astype(BF16)

    take(LZ.at[pl.ds(0, NZ - 1)], ssem.at[4])
    LY[y] = jnp.sum(LZ[...], axis=0)

    for i in (0, 1):
        take(YR.at[i], ysem.at[i])
        stage(2 + i, GW[i, :, cols(yr)] + YR[i].astype(F32))
        take(YR.at[6 + i], ysem.at[6 + i])
        stage(8 + i, GW[2 + i, :, cols(yl)] + YR[6 + i].astype(F32))
        put(YS.at[2 + i], YR.at[2 + i], sends.at[11], ysem.at[2 + i], {"y": yr})
        put(YS.at[8 + i], YR.at[8 + i], sends.at[11], ysem.at[8 + i], {"y": yl})
    for i in range(1, NY):
        put(LY.at[y], LY.at[y], sends.at[12], ssem.at[5], {"y": lax.rem(y + i, NY)})
    for q, (one, two) in enumerate(((2, 10), (3, 11), (8, 4), (9, 5))):
        take(YR.at[one], ysem.at[one])
        take(YR.at[two], ysem.at[two])
        value = GW[q, :, cols(y)] + YR[one].astype(F32) + YR[two].astype(F32)
        gw_out[pl.ds(q * 128, 128), :] = value.astype(BF16)

    take(LY.at[pl.ds(0, NY - 1)], ssem.at[5])
    loss_out[0, 0] = jnp.sum(jnp.sum(LY[...], axis=0)[:, 0:1])

    take(INFO.at[pl.ds(0, NZ - 1)], sends.at[0])
    take(GR.at[pl.ds(0, 2 * NZ - 1)], sends.at[1])
    take(W.at[pl.ds(0, 2)], sends.at[2])
    take(STA.at[pl.ds(0, 3)], sends.at[3])
    take(INFO.at[pl.ds(0, (NY - 1) * NZ)], sends.at[4])
    take(W.at[0], sends.at[5])
    take(GR.at[pl.ds(0, 6 * NZ)], sends.at[6])
    take(GR.at[pl.ds(0, 8 * NZ)], sends.at[7])
    take(SB.at[pl.ds(0, NZ - 1)], sends.at[8])
    take(STB.at[pl.ds(0, NX - 1)], sends.at[9])
    take(LZ.at[pl.ds(0, NZ - 1)], sends.at[10])
    take(YR, sends.at[11])
    take(LY.at[pl.ds(0, NY - 1)], sends.at[12])
    for side, away, ok in ((0, -1, k < NZ - 1), (1, 1, k > 0)):
        for hop in range(NZ):
            origin = k + away * hop
            pl.when((origin >= 0) & (origin < NZ) & ok)(
                lambda side=side, hop=hop: take(MX.at[:, pl.ds(0, rows)], mssem.at[side, hop])
            )


def shards(logits, targets, resp_mask, rewards, groups, unit_grad, mix, w_out):
    rows, vocab = logits.shape
    heads, depth = w_out.shape
    sub = unit_grad.shape[0]
    vmem = pl.BlockSpec(memory_space=pltpu.VMEM)
    smem = pl.BlockSpec(memory_space=pltpu.SMEM)
    hbm = pl.BlockSpec(memory_space=pltpu.HBM)
    dma = pltpu.SemaphoreType.DMA
    logprob, loss, grad_mix, grad_w = pl.pallas_call(
        kernel,
        name="step",
        out_shape=(
            jax.ShapeDtypeStruct((1, rows), F32),
            jax.ShapeDtypeStruct((1, 1), F32),
            jax.ShapeDtypeStruct((rows, heads), BF16),
            jax.ShapeDtypeStruct((heads, depth), BF16),
        ),
        in_specs=[hbm, vmem, vmem, smem, smem, hbm, hbm, hbm],
        out_specs=(vmem, smem, vmem, vmem),
        scratch_shapes=[
            pltpu.VMEM((rows, vocab), BF16),
            pltpu.VMEM((NZ, sub, NY * depth), BF16),
            pltpu.VMEM((NX * 2 * NZ * 2, sub, NY * depth), BF16),
            pltpu.VMEM((SUB, NZ * rows, heads // SUB), BF16),
            pltpu.VMEM((NY, heads, depth), BF16),
            pltpu.VMEM((NZ * rows, NY * depth), BF16),
            pltpu.VMEM((NZ, rows, heads), F32),
            pltpu.VMEM((2, NZ, rows, heads), BF16),
            pltpu.VMEM((NZ, rows, heads), BF16),
            pltpu.VMEM((SUB, heads // SUB, NY * depth), F32),
            pltpu.VMEM((12, heads // SUB, depth), BF16),
            pltpu.VMEM((12, heads // SUB, depth), BF16),
            pltpu.VMEM((NY * NZ, 1, 128), F32),
            pltpu.VMEM((NZ, 1, 128), F32),
            pltpu.VMEM((NZ, 1, 128), F32),
            pltpu.VMEM((4, 8, 128), F32),
            pltpu.VMEM((NX, 8, 128), F32),
            pltpu.VMEM((NZ, 1, 128), F32),
            pltpu.VMEM((NY, 1, 128), F32),
            dma((4,)), dma((NZ,)), dma((4, NZ)), dma((NZ,)), dma((NZ, SUB)), dma((6,)),
            dma((2, NZ, SUB)), dma((12,)), dma((6,)), dma((2, NZ)), dma((13,)),
        ],
        compiler_params=pltpu.CompilerParams(
            collective_id=0, has_side_effects=True, vmem_limit_bytes=58 * 1024 * 1024
        ),
    )(
        logits, targets.reshape(1, rows), resp_mask.reshape(1, rows), rewards, groups,
        unit_grad, mix, w_out,
    )
    return logprob.reshape(rows), loss.reshape(()), grad_mix, grad_w


def solution(mesh):
    finer = Mesh(mesh.devices.reshape(NY, NZ, NX, 2, 2), DP + MP)
    in_specs = (
        P(DP, MP), P(DP), P(DP), P(DP), P(DP), P(DP + MP, None), P(DP, MP), P(MP, DP)
    )
    out_specs = (P(DP), P(), P(DP, MP), P(MP, DP))
    return jax.shard_map(
        shards, mesh=finer, in_specs=in_specs, out_specs=out_specs, check_vma=False
    )
```

time: 449 us -> 92.7 us (0.21)
  the two profiles are of different devices: /device:TPU:4 before, /device:TPU:32 now
where the time goes in v2:
time: 92.7 us; the launch traced here: 92.5 us
  Pallas kernels  85.4 us (92%)
  between operations  3.65 us (4%)
  local copies, waits for them, and re-layouts  3.51 us (4%)
    pallas_call x1, Pallas kernels, shards(): pl.pallas_call(kernel, name='step', out_shape=(jax.ShapeDtypeStruct((1, r...  85.4 us
    unnamed x5, local copies, waits for them, and re-layouts  3.51 us

profile of v2, /device:TPU:32, one launch (start us, length us, event | category | flops | bytes accessed | tf_op | source)
XLA Modules:
  0.0 92.5 jit_solution(8108693768987691335)
XLA Ops:
  1.9 85.4 %step.1 = (f32[1,128]{1,0:T(1,128)}, f32[1,1]{1,0:T(1,128)}, bf16[128,512]{1,0:T(8,128)(2,1)}, bf16[512,256]{1,0:T(8,128)(2,1)}) custom-call(bf16[128,4096]{1,0:T(8,128)(2,1)} %logits.1, s32[1,128]{1,0:T(1,128)} %bitcast.4, s32[1,128]{1,0:T(1,128)} %bitcast.5, s32[1]{0:T(128)S(6)} %copy.16.rewards, s32[1]{0:T(128)S(6)} %copy.17.groups, bf16[8,8192]{1,0:T(8,128)(2,1)} %ug.1, ...), custom_call_target="tpu_custom_call" | custom-call | tf_op jit(solution)/shard_map/step/pallas_call | solution.py:444
  87.3 0.0 copy-start
  87.3 1.2 %copy.18 = f32[128]{0:T(128)} copy(f32[128]{0:T(128)} %bitcast.6) | data formatting | bytes 1024
  89.1 1.6 %copy.20 = bf16[128,512]{1,0:T(8,128)(2,1)} copy(bf16[128,512]{1,0:T(8,128)(2,1)} %get-tuple-element.18) | data formatting | bytes 262144
  90.7 0.0 copy-done
  90.7 0.7 copy.21
Async XLA Ops:
  87.3 3.4 %copy-start = (bf16[512,256]{1,0:T(8,128)(2,1)S(1)}, bf16[512,256]{1,0:T(8,128)(2,1)}, u32[]{:S(2)}) copy-start(bf16[512,256]{1,0:T(8,128)(2,1)} %get-tuple-element.19) | copy-start | bytes 786436

commit v3 on v2

v3 whole, which is shorter than its diff:
```python
import jax
import jax.numpy as jnp
from jax import lax
from jax.experimental import pallas as pl
from jax.experimental.pallas import tpu as pltpu
from jax.sharding import Mesh
from jax.sharding import PartitionSpec as P

K = 4
NY, NZ, NX = 4, 8, 4
DP = ("y", "zl")
MP = ("x", "zh", "core")
F32, BF16 = jnp.float32, jnp.bfloat16
NT = (((1,), (1,)), ((), ()))
TN = (((0,), (0,)), ((), ()))
SUB = 4
LAG, SKEW = 3, 2


def kernel(
    logits, targets, mask, rewards, groups, ug, mix, w_out,
    lp_out, loss_out, gmix_out, gw_out,
    LG, UV, US, GR, MX, W, G2, PF, RB, SB, GW, YS, YR, INFO, GRP, REW, WSC, LSC, STA, STB, LZ, LY,
    lsem, zsem, xsem, dsem, msem, wsem, rsem, ysem, ssem, mssem, sends,
):
    y, k, x = lax.axis_index("y"), lax.axis_index("zl"), lax.axis_index("x")
    h, c = lax.axis_index("zh"), lax.axis_index("core")
    rows, vocab = LG.shape
    depth = W.shape[2]
    xr, xl = lax.rem(x + 1, NX), lax.rem(x + NX - 1, NX)
    xo = lax.rem(x + 2, NX)
    yr, yl = lax.rem(y + 1, NY), lax.rem(y + NY - 1, NY)
    yo = lax.rem(y + 2, NY)
    right, left, opp = {"zl": k + 1}, {"zl": k - 1}, {"core": 1 - c}

    def idx(xx, cc, zz, hh):
        return ((xx * 2 + cc) * NZ + zz) * 2 + hh

    def unit(xx, cc, zz):
        return GR.at[pl.ds(idx(xx, cc, zz, 0), 2)]

    def put(src, dst, send, recv, where):
        pltpu.make_async_remote_copy(
            src_ref=src, dst_ref=dst, send_sem=send, recv_sem=recv,
            device_id=where, device_id_type=pl.DeviceIdType.MESH,
        ).start()

    def take(ref, sem):
        pltpu.make_async_copy(ref, ref, sem).wait()

    def cols(i):
        return pl.ds(pl.multiple_of(i * depth, depth), depth)

    load_rows = pltpu.make_async_copy(ug, UV, lsem.at[1])
    load_rows.start()

    barrier = pltpu.get_barrier_semaphore()
    peers = []
    for step in range(1, 2 * NZ):
        place = lax.rem(h * NZ + k + step, 2 * NZ)
        peers.append({"zh": place // NZ, "zl": lax.rem(place, NZ)})
    peers += [{"y": lax.rem(y + i, NY)} for i in range(1, NY)]
    peers += [{"x": lax.rem(x + i, NX)} for i in range(1, NX)]
    peers += [opp, {"zh": 1 - h, "core": 1 - c}]
    for peer in peers:
        pl.semaphore_signal(barrier, inc=1, device_id=peer, device_id_type=pl.DeviceIdType.MESH)

    load_w = pltpu.make_async_copy(w_out, W.at[y], lsem.at[3])
    load_w.start()
    own_rows = pl.ds(pl.multiple_of(k * rows, rows), rows)
    for q in range(SUB):
        pltpu.make_async_copy(
            mix.at[:, pl.ds(q * 128, 128)], MX.at[q, own_rows], lsem.at[2]
        ).start()
    load_logits = pltpu.make_async_copy(logits, LG, lsem.at[0])
    load_logits.start()
    for yy in range(NY):
        pltpu.make_async_copy(
            ug.at[:, cols(yy * NZ + k)],
            GR.at[idx(x, c, k, h), :, pl.ds(yy * depth, depth)], zsem.at[k],
        ).start()

    lane = lax.broadcasted_iota(jnp.int32, (1, 128), 1)
    length = jnp.sum(mask[...].astype(F32), axis=1, keepdims=True)
    facts = jnp.where(lane == 0, jnp.broadcast_to(rewards[...].astype(F32), (1, 128)), 0.0)
    facts = facts + jnp.where(lane == 1, jnp.broadcast_to(groups[...].astype(F32), (1, 128)), 0.0)
    facts = facts + jnp.where(lane == 2, jnp.broadcast_to(length, (1, 128)), 0.0)
    me = y * NZ + k
    INFO[me] = facts

    load_rows.wait()
    for zz in range(NZ):
        for yy in range(NY):
            US[zz, :, yy * depth : (yy + 1) * depth] = UV[
                :, (yy * NZ + zz) * depth : (yy * NZ + zz + 1) * depth
            ]
    pl.semaphore_wait(barrier, len(peers))

    for i in range(1, NZ):
        put(INFO.at[me], INFO.at[me], sends.at[0], ssem.at[0], {"zl": lax.rem(k + i, NZ)})
    mine = idx(x, c, k, h)
    for far in range(NZ - 1, -1, -1):
        for side in (1, -1) if far else (1,):
            to = k + side * far

            def send_rows(to=to, far=far):
                for hh in (0, 1):
                    if far == 0 and hh == 0:
                        continue
                    zh = hh if far else 1 - h
                    put(US.at[to], GR.at[mine], sends.at[1], zsem.at[k], {"zl": to, "zh": zh})

            if far == 0:
                send_rows()
            else:
                pl.when((to >= 0) & (to < NZ))(send_rows)
    half = W.shape[1] // 2
    first, second = pl.ds(0, half), pl.ds(half, half)
    load_w.wait()
    put(W.at[y, first], W.at[y, first], sends.at[2], wsem.at[0], {"y": yr})
    put(W.at[y, second], W.at[y, second], sends.at[2], wsem.at[3], {"y": yl})
    put(W.at[y, second], W.at[y, second], sends.at[2], wsem.at[1], {"y": yr})
    put(W.at[y, first], W.at[y, first], sends.at[2], wsem.at[4], {"y": yl})

    step_rows = rows // SUB

    def mix_at(zz, q):
        return MX.at[q, pl.ds(pl.multiple_of(zz * rows, rows), rows)]

    def forward(hop, q):
        for side, away, ok in ((0, -1, k < NZ - 1), (1, 1, k > 0)):
            origin = k + away * hop

            def one(side=side, origin=origin, ok=ok):
                @pl.when(hop > 0)
                def _():
                    take(mix_at(origin, q), msem.at[origin, q])

                @pl.when(ok)
                def _():
                    put(
                        mix_at(origin, q), mix_at(origin, q), mssem.at[side, hop],
                        msem.at[origin, q], (right, left)[side],
                    )

            pl.when((hop >= 0) & (hop < NZ) & (origin >= 0) & (origin < NZ))(one)

    def z_step(t):
        s = t - LAG
        going = (
            (0, NZ - 1 - (s - k), (s >= k) & (s < NZ - 1), k > 0),
            (1, s - (NZ - 1 - k), (s >= NZ - 1 - k) & (s < NZ - 1), k < NZ - 1),
        )

        def one(q, carry):
            part = pl.ds(pl.multiple_of(q * step_rows, step_rows), step_rows)
            for side, to, ok, more in going:

                def store(side=side, to=to, more=more):
                    @pl.when(more)
                    def _():
                        take(RB.at[side, to, part], rsem.at[side, to, q])
                        SB[to, part, :] = (PF[to, part, :] + RB[side, to, part, :].astype(F32)).astype(BF16)

                    @pl.when(jnp.logical_not(more))
                    def _():
                        SB[to, part, :] = PF[to, part, :].astype(BF16)

                pl.when(ok)(store)
            forward(t - SKEW * (q // 2), q)
            for side, to, ok, more in going:

                def send(side=side, to=to):
                    put(
                        SB.at[to, part], RB.at[side, to, part], sends.at[8],
                        rsem.at[side, to, q], (right, left)[side],
                    )

                pl.when(ok)(send)
            return carry

        lax.fori_loop(0, SUB, one, 0)

    take(MX.at[:, own_rows], lsem.at[2])
    z_step(0)

    load_logits.wait()
    eye = lax.broadcasted_iota(jnp.int32, (rows, rows), 0) == lax.broadcasted_iota(
        jnp.int32, (rows, rows), 1
    )
    column = lax.broadcasted_iota(jnp.int32, (rows, 128), 1).astype(F32)
    shift = ((x * 2 + h) * 2 + c) * vocab
    wanted = (targets[...] - shift).astype(F32)
    wanted = jnp.sum(jnp.where(eye, wanted, 0.0), axis=1, keepdims=True)

    def piece(j):
        return LG[:, pl.ds(pl.multiple_of(j * 128, 128), 128)].astype(F32)

    tiles = vocab // 128
    peak = lax.fori_loop(
        0, tiles, lambda j, m: jnp.maximum(m, piece(j)), jnp.full((rows, 128), -jnp.inf, F32)
    )
    peak = jnp.max(peak, axis=1, keepdims=True)

    def collect(j, carry):
        total, found = carry
        value = piece(j)
        total = total + jnp.exp(value - peak)
        at = wanted - (j * 128).astype(F32)
        return total, found + jnp.where(column == at, value, 0.0)

    zero = jnp.zeros((rows, 128), F32)
    total, found = lax.fori_loop(0, tiles, collect, (zero, zero))

    def as_row(v):
        return jnp.sum(jnp.where(eye, v, 0.0), axis=0, keepdims=True)

    a = h * 2 + c
    STA[a, 0:1, :] = as_row(peak)
    STA[a, 1:2, :] = as_row(jnp.sum(total, axis=1, keepdims=True))
    STA[a, 2:3, :] = as_row(jnp.sum(found, axis=1, keepdims=True))

    take(INFO.at[pl.ds(0, NZ - 1)], ssem.at[0])
    line = INFO.at[pl.ds(y * NZ, NZ)]
    for i in range(1, NY):
        put(line, line, sends.at[4], ssem.at[1], {"y": lax.rem(y + i, NY)})
    for peer in ({"zh": 1 - h}, opp, {"zh": 1 - h, "core": 1 - c}):
        put(STA.at[a], STA.at[a], sends.at[3], ssem.at[2], peer)

    take(W.at[yl, first], wsem.at[0])
    put(W.at[yl, first], W.at[yl, first], sends.at[5], wsem.at[2], {"y": yr})
    take(W.at[yr, second], wsem.at[3])
    put(W.at[yr, second], W.at[yr, second], sends.at[5], wsem.at[5], {"y": yl})

    def weights():
        take(INFO.at[pl.ds(0, (NY - 1) * NZ)], ssem.at[1])
        count = jnp.zeros((1, 128), F32)
        for r in range(NY * NZ):
            fact = INFO[r]
            count = count + fact
            GRP[r] = jnp.broadcast_to(fact[:, 1:2], (1, 128))
            REW[r] = jnp.broadcast_to(fact[:, 0:1], (1, 128))
        count = jnp.broadcast_to(count[:, 2:3], (1, 128))

        def weigh(zz, carry):
            reward, group = REW[y * NZ + zz], GRP[y * NZ + zz]
            own = jnp.zeros((1, 128), F32)
            for r in range(NY * NZ):
                own = own + jnp.where(GRP[r] == group, REW[r], 0.0)
            WSC[zz] = (reward - (own - reward) / (K - 1)) / count
            LSC[zz] = jnp.broadcast_to(INFO[y * NZ + zz][:, 2:3], (1, 128))
            return carry

        lax.fori_loop(0, NZ, weigh, 0)

    def merge(ref, n):
        top = ref[0, 0:1, :]
        for i in range(1, n):
            top = jnp.maximum(top, ref[i, 0:1, :])
        total = jnp.zeros_like(top)
        found = jnp.zeros_like(top)
        for i in range(n):
            total = total + ref[i, 1:2, :] * jnp.exp(ref[i, 0:1, :] - top)
            found = found + ref[i, 2:3, :]
        return top, total, found

    def join_stats():
        take(STA.at[pl.ds(0, 3)], ssem.at[2])
        for i, v in enumerate(merge(STA, 4)):
            STB[x, i : i + 1, :] = v
        for i in range(1, NX):
            put(STB.at[x], STB.at[x], sends.at[9], ssem.at[3], {"x": lax.rem(x + i, NX)})

    def arrived(zz):
        take(unit(x, c, zz), zsem.at[zz])
        here = unit(x, c, zz)
        put(here, here, sends.at[6], xsem.at[0, zz], {"x": xr})
        put(here, here, sends.at[6], xsem.at[1, zz], {"x": xl})
        put(here, here, sends.at[7], dsem.at[zz], opp)

    def passed(zz):
        for side, origin, to in ((0, xl, xr), (1, xr, xl)):
            here = unit(origin, c, zz)
            take(here, xsem.at[side, zz])
            part = GR.at[idx(origin, c, zz, side)]
            put(part, part, sends.at[6], xsem.at[2 + side, zz], {"x": to})
            put(here, here, sends.at[7], dsem.at[zz], opp)

    def closed(zz):
        for side in (0, 1):
            take(GR.at[idx(xo, c, zz, side)], xsem.at[2 + side, zz])
        here = unit(xo, c, zz)
        put(here, here, sends.at[7], dsem.at[zz], opp)

    def scaled(zz):
        take(GR.at[pl.ds(0, 8)], dsem.at[zz])
        weight, limit = WSC[zz], LSC[zz]
        base = pl.multiple_of(zz * rows, rows)

        def scale(i, carry):
            xx, hh = i // 2, lax.rem(i, 2)
            pair = jnp.concatenate(
                [GR[idx(xx, cc, zz, hh)].astype(F32) for cc in (0, 1)], axis=0
            )
            place = (lax.broadcasted_iota(jnp.int32, (16, 128), 0) + i * 16).astype(F32)
            factor = jnp.where(place < limit, -weight, 0.0)
            factor = jnp.concatenate([factor] * (pair.shape[1] // 128), axis=1)
            G2[pl.ds(pl.multiple_of(base + i * 16, 16), 16), :] = (factor * pair).astype(BF16)
            return carry

        lax.fori_loop(0, rows // 16, scale, 0)

    def partial(zz):
        block = G2[pl.ds(pl.multiple_of(zz * rows, rows), rows), :]
        acc = None
        for yy in range(NY):
            one = lax.dot_general(
                block[:, yy * depth : (yy + 1) * depth], W[yy], NT, preferred_element_type=F32
            )
            acc = one if acc is None else acc + one
        PF[zz] = acc

    def both(far, act):
        for side in (1, -1):
            zz = k + side * far
            ok = (zz >= 0) & (zz < NZ) & (far >= 0) & (far < NZ)
            if side == -1:
                ok = ok & (far > 0)

            pl.when(ok)(lambda zz=zz: act(zz))

    def lines(turn, act):
        both(NZ - 1 - 2 * turn, act)
        both(NZ - 2 - 2 * turn, act)

    def step(t, carry):
        lines(t, arrived)
        lines(t - 1, passed)
        lines(t - 2, closed)

        @pl.when(t == 2)
        def _():
            weights()
            take(W.at[yl, second], wsem.at[1])
            take(W.at[yr, first], wsem.at[4])
            take(W.at[yo, first], wsem.at[2])
            take(W.at[yo, second], wsem.at[5])

        lines(t - LAG, scaled)
        both(NZ - 1 - (t - LAG), partial)
        pl.when(t > 0)(lambda: z_step(t))
        pl.when(t == 5)(join_stats)
        return carry

    def product(q):
        value = lax.dot_general(MX[q], G2[...], TN, preferred_element_type=F32)
        for yy in range(NY):
            GW[q, yy] = value[:, yy * depth : (yy + 1) * depth]

    def stage(slot, value):
        YS[slot] = value.astype(BF16)

    def pass_on(slot, where):
        put(YS.at[slot], YR.at[slot], sends.at[11], ysem.at[slot], where)

    to_right, to_left = {"y": yr}, {"y": yl}

    def y_first(pair):
        p, q = 2 * pair, 6 * pair
        product(p)
        stage(q, GW[p, yo])
        product(p + 1)
        pass_on(q, to_right)
        stage(q + 1, GW[p + 1, yo])
        stage(q + 4, GW[p + 1, yr])
        pass_on(q + 1, to_left)
        stage(q + 5, GW[p, yl])
        pass_on(q + 4, to_right)
        pass_on(q + 5, to_left)

    def y_second(pair):
        p, q = 2 * pair, 6 * pair
        take(YR.at[q], ysem.at[q])
        stage(q + 2, GW[p, yr] + YR[q].astype(F32))
        take(YR.at[q + 1], ysem.at[q + 1])
        pass_on(q + 2, to_right)
        stage(q + 3, GW[p + 1, yl] + YR[q + 1].astype(F32))
        pass_on(q + 3, to_left)

    def y_third(pair):
        q = 6 * pair
        for p, one, two in ((2 * pair, q + 2, q + 5), (2 * pair + 1, q + 3, q + 4)):
            take(YR.at[two], ysem.at[two])
            take(YR.at[one], ysem.at[one])
            value = GW[p, y] + YR[one].astype(F32) + YR[two].astype(F32)
            gw_out[pl.ds(p * 128, 128), :] = value.astype(BF16)

    lax.fori_loop(0, NZ, step, 0)
    y_first(0)
    lax.fori_loop(NZ, NZ + 1, step, 0)
    y_second(0)

    take(STB.at[pl.ds(0, NX - 1)], ssem.at[3])
    top, total, found = merge(STB, NX)
    logprob = found - (top + jnp.log(total))
    lp_out[...] = logprob
    weight = jnp.where(lane.astype(F32) < LSC[k], WSC[k], 0.0)
    LZ[k] = jnp.broadcast_to(-jnp.sum(weight * logprob, axis=1, keepdims=True), (1, 128))

    lax.fori_loop(NZ + 1, NZ + SKEW, step, 0)
    for i in range(1, NZ):
        put(LZ.at[k], LZ.at[k], sends.at[10], ssem.at[4], {"zl": lax.rem(k + i, NZ)})
    y_first(1)
    partial(k)
    y_third(0)

    def add_side(side):
        for q in range(SUB):
            part = pl.ds(q * step_rows, step_rows)
            take(RB.at[side, k, part], rsem.at[side, k, q])
        PF[k] = PF[k] + RB[side, k].astype(F32)

    pl.when(k > 0)(lambda: add_side(0))
    pl.when(k < NZ - 1)(lambda: add_side(1))
    gmix_out[...] = PF[k].astype(BF16)

    y_second(1)
    take(LZ.at[pl.ds(0, NZ - 1)], ssem.at[4])
    LY[y] = jnp.sum(LZ[...], axis=0)
    for i in range(1, NY):
        put(LY.at[y], LY.at[y], sends.at[12], ssem.at[5], {"y": lax.rem(y + i, NY)})
    y_third(1)
    take(LY.at[pl.ds(0, NY - 1)], ssem.at[5])
    loss_out[...] = jnp.sum(LY[...], axis=0)

    take(INFO.at[pl.ds(0, NZ - 1)], sends.at[0])
    take(GR.at[pl.ds(0, 2 * NZ - 1)], sends.at[1])
    take(W.at[pl.ds(0, 2)], sends.at[2])
    take(STA.at[pl.ds(0, 3)], sends.at[3])
    take(INFO.at[pl.ds(0, (NY - 1) * NZ)], sends.at[4])
    take(W.at[0], sends.at[5])
    take(GR.at[pl.ds(0, 6 * NZ)], sends.at[6])
    take(GR.at[pl.ds(0, 8 * NZ)], sends.at[7])
    take(SB.at[pl.ds(0, NZ - 1)], sends.at[8])
    take(STB.at[pl.ds(0, NX - 1)], sends.at[9])
    take(LZ.at[pl.ds(0, NZ - 1)], sends.at[10])
    take(YR, sends.at[11])
    take(LY.at[pl.ds(0, NY - 1)], sends.at[12])
    for side, away, ok in ((0, -1, k < NZ - 1), (1, 1, k > 0)):
        for hop in range(NZ):
            origin = k + away * hop
            pl.when((origin >= 0) & (origin < NZ) & ok)(
                lambda side=side, hop=hop: take(MX.at[:, pl.ds(0, rows)], mssem.at[side, hop])
            )


def finish(lp, loss, gmix, gw, lp_out, loss_out, gmix_out, gw_out):
    lp_out[...] = lp[...]
    loss_out[0, 0] = jnp.sum(loss[:, 0:1])
    gmix_out[...] = gmix[...]
    gw_out[...] = gw[...]


def shards(logits, targets, resp_mask, rewards, groups, unit_grad, mix, w_out):
    rows, vocab = logits.shape
    heads, depth = w_out.shape
    sub = unit_grad.shape[0]
    vmem = pl.BlockSpec(memory_space=pltpu.VMEM)
    smem = pl.BlockSpec(memory_space=pltpu.SMEM)
    hbm = pl.BlockSpec(memory_space=pltpu.HBM)
    dma = pltpu.SemaphoreType.DMA
    logprob, loss, grad_mix, grad_w = pl.pallas_call(
        kernel,
        name="step",
        out_shape=(
            jax.ShapeDtypeStruct((1, rows), F32),
            jax.ShapeDtypeStruct((1, 128), F32),
            jax.ShapeDtypeStruct((rows, heads), BF16),
            jax.ShapeDtypeStruct((heads, depth), BF16),
        ),
        in_specs=[hbm, vmem, vmem, vmem, vmem, hbm, hbm, hbm],
        out_specs=(vmem, vmem, vmem, vmem),
        scratch_shapes=[
            pltpu.VMEM((rows, vocab), BF16),
            pltpu.VMEM((sub, NY * NZ * depth), BF16),
            pltpu.VMEM((NZ, sub, NY * depth), BF16),
            pltpu.VMEM((NX * 2 * NZ * 2, sub, NY * depth), BF16),
            pltpu.VMEM((SUB, NZ * rows, heads // SUB), BF16),
            pltpu.VMEM((NY, heads, depth), BF16),
            pltpu.VMEM((NZ * rows, NY * depth), BF16),
            pltpu.VMEM((NZ, rows, heads), F32),
            pltpu.VMEM((2, NZ, rows, heads), BF16),
            pltpu.VMEM((NZ, rows, heads), BF16),
            pltpu.VMEM((SUB, NY, heads // SUB, depth), F32),
            pltpu.VMEM((12, heads // SUB, depth), BF16),
            pltpu.VMEM((12, heads // SUB, depth), BF16),
            pltpu.VMEM((NY * NZ, 1, 128), F32),
            pltpu.VMEM((NY * NZ, 1, 128), F32),
            pltpu.VMEM((NY * NZ, 1, 128), F32),
            pltpu.VMEM((NZ, 1, 128), F32),
            pltpu.VMEM((NZ, 1, 128), F32),
            pltpu.VMEM((4, 8, 128), F32),
            pltpu.VMEM((NX, 8, 128), F32),
            pltpu.VMEM((NZ, 1, 128), F32),
            pltpu.VMEM((NY, 1, 128), F32),
            dma((4,)), dma((NZ,)), dma((4, NZ)), dma((NZ,)), dma((NZ, SUB)), dma((6,)),
            dma((2, NZ, SUB)), dma((12,)), dma((6,)), dma((2, NZ)), dma((13,)),
        ],
        compiler_params=pltpu.CompilerParams(
            collective_id=0, has_side_effects=True, vmem_limit_bytes=58 * 1024 * 1024
        ),
    )(
        logits, targets.reshape(1, rows), resp_mask.reshape(1, rows),
        rewards.reshape(1, 1), groups.reshape(1, 1),
        unit_grad, mix, w_out,
    )
    logprob, loss, grad_mix, grad_w = pl.pallas_call(
        finish,
        name="finish",
        out_shape=(
            jax.ShapeDtypeStruct((1, rows), F32),
            jax.ShapeDtypeStruct((1, 1), F32),
            jax.ShapeDtypeStruct((rows, heads), BF16),
            jax.ShapeDtypeStruct((heads, depth), BF16),
        ),
        in_specs=[vmem] * 4,
        out_specs=(vmem, smem, vmem, vmem),
    )(logprob, loss, grad_mix, grad_w)
    return logprob.reshape(rows), loss.reshape(()), grad_mix, grad_w


def solution(mesh):
    finer = Mesh(mesh.devices.reshape(NY, NZ, NX, 2, 2), DP + MP)
    in_specs = (
        P(DP, MP), P(DP), P(DP), P(DP), P(DP), P(DP + MP, None), P(DP, MP), P(MP, DP)
    )
    out_specs = (P(DP), P(), P(DP, MP), P(MP, DP))
    return jax.shard_map(
        shards, mesh=finer, in_specs=in_specs, out_specs=out_specs, check_vma=False
    )
```

time: 92.7 us -> 76.6 us (0.83)
  the two profiles are of different devices: /device:TPU:32 before, /device:TPU:4 now
where the time goes in v3:
time: 76.6 us; the launch traced here: 76.4 us
  Pallas kernels  74.5 us (97%)
  between operations  1.93 us (3%)
    pallas_call x1, Pallas kernels, shards(): pl.pallas_call(kernel, name='step', out_shape=(jax.ShapeDtypeStruct((1, r...  72.7 us
    pallas_call x1, Pallas kernels, shards(): pl.pallas_call(finish, name='finish', out_shape=(jax.ShapeDtypeStruct((1,...  1.8 us

profile of v3, /device:TPU:4, one launch (start us, length us, event | category | flops | bytes accessed | tf_op | source)
XLA Modules:
  0.0 76.4 jit_solution(3820986399118677700)
XLA Ops:
  1.9 72.7 %step.1 = (f32[1,128]{1,0:T(1,128)}, f32[1,128]{1,0:T(1,128)}, bf16[128,512]{1,0:T(8,128)(2,1)}, bf16[512,256]{1,0:T(8,128)(2,1)}) custom-call(bf16[128,4096]{1,0:T(8,128)(2,1)} %logits.1, s32[1,128]{1,0:T(1,128)} %bitcast.8, s32[1,128]{1,0:T(1,128)} %bitcast.9, s32[1,1]{1,0:T(1,128)} %bitcast.6.rewards, s32[1,1]{1,0:T(1,128)} %bitcast.7.groups, ...), custom_call_target="tpu_custom_call" | custom-call | tf_op jit(solution)/shard_map/step/pallas_call | solution.py:472
  74.6 1.8 %finish.1 = (f32[1,128]{1,0:T(1,128)}, f32[1,1]{1,0:T(1,128)}, bf16[128,512]{1,0:T(8,128)(2,1)}, bf16[512,256]{1,0:T(8,128)(2,1)}) custom-call(f32[1,128]{1,0:T(1,128)} %get-tuple-element.12.lp, f32[1,128]{1,0:T(1,128)} %get-tuple-element.13.loss, bf16[128,512]{1,0:T(8,128)(2,1)} %get-tuple-element.14.gmix, bf16[512,256]{1,0:T(8,128)(2,1)} %get-tuple-element.15.gw), custom_call_target="tpu_custom_call" | custom-call | tf_op jit(solution)/shard_map/finish/pallas_call | solution.py:517

commit v4 on v3

--- a/solution.py
+++ b/solution.py
@@ -14,7 +14,9 @@
 NT = (((1,), (1,)), ((), ()))
 TN = (((0,), (0,)), ((), ()))
 SUB = 4
-LAG, SKEW = 3, 2
+LAG, OFF, SKEW, CUT = 3, 1, 1, 3
+SCALE_AT = (3, 4, 5, 6)
+JOIN_AT = 4
 
 
 def kernel(
@@ -127,7 +129,7 @@
     def mix_at(zz, q):
         return MX.at[q, pl.ds(pl.multiple_of(zz * rows, rows), rows)]
 
-    def forward(hop, q):
+    def forward(hop, q, least):
         for side, away, ok in ((0, -1, k < NZ - 1), (1, 1, k > 0)):
             origin = k + away * hop
 
@@ -143,7 +145,7 @@
                         msem.at[origin, q], (right, left)[side],
                     )
 
-            pl.when((hop >= 0) & (hop < NZ) & (origin >= 0) & (origin < NZ))(one)
+            pl.when((hop >= least) & (hop < NZ) & (origin >= 0) & (origin < NZ))(one)
 
     def z_step(t):
         s = t - LAG
@@ -167,7 +169,7 @@
                         SB[to, part, :] = PF[to, part, :].astype(BF16)
 
                 pl.when(ok)(store)
-            forward(t - SKEW * (q // 2), q)
+            forward(t - OFF - SKEW * (q // CUT), q, 1)
             for side, to, ok, more in going:
 
                 def send(side=side, to=to):
@@ -182,7 +184,14 @@
         lax.fori_loop(0, SUB, one, 0)
 
     take(MX.at[:, own_rows], lsem.at[2])
-    z_step(0)
+    def own(q, carry):
+        forward(0, q, 0)
+        return carry
+
+    def own_blocks():
+        lax.fori_loop(0, SUB, own, 0)
+
+    own_blocks()
 
     load_logits.wait()
     eye = lax.broadcasted_iota(jnp.int32, (rows, rows), 0) == lax.broadcasted_iota(
@@ -334,22 +343,23 @@
         both(NZ - 2 - 2 * turn, act)
 
     def step(t, carry):
+        pl.when(t == 1)(weights)
         lines(t, arrived)
         lines(t - 1, passed)
         lines(t - 2, closed)
 
         @pl.when(t == 2)
         def _():
-            weights()
             take(W.at[yl, second], wsem.at[1])
             take(W.at[yr, first], wsem.at[4])
             take(W.at[yo, first], wsem.at[2])
             take(W.at[yo, second], wsem.at[5])
 
-        lines(t - LAG, scaled)
+        for turn, when in enumerate(SCALE_AT):
+            pl.when(t == when)(lambda turn=turn: lines(turn, scaled))
         both(NZ - 1 - (t - LAG), partial)
-        pl.when(t > 0)(lambda: z_step(t))
-        pl.when(t == 5)(join_stats)
+        z_step(t)
+        pl.when(t == JOIN_AT)(join_stats)
         return carry
 
     def product(q):
@@ -365,54 +375,54 @@
 
     to_right, to_left = {"y": yr}, {"y": yl}
 
-    def y_first(pair):
-        p, q = 2 * pair, 6 * pair
-        product(p)
-        stage(q, GW[p, yo])
-        product(p + 1)
-        pass_on(q, to_right)
-        stage(q + 1, GW[p + 1, yo])
-        stage(q + 4, GW[p + 1, yr])
-        pass_on(q + 1, to_left)
-        stage(q + 5, GW[p, yl])
-        pass_on(q + 4, to_right)
-        pass_on(q + 5, to_left)
-
-    def y_second(pair):
-        p, q = 2 * pair, 6 * pair
-        take(YR.at[q], ysem.at[q])
-        stage(q + 2, GW[p, yr] + YR[q].astype(F32))
-        take(YR.at[q + 1], ysem.at[q + 1])
-        pass_on(q + 2, to_right)
-        stage(q + 3, GW[p + 1, yl] + YR[q + 1].astype(F32))
-        pass_on(q + 3, to_left)
-
-    def y_third(pair):
-        q = 6 * pair
-        for p, one, two in ((2 * pair, q + 2, q + 5), (2 * pair + 1, q + 3, q + 4)):
+    top_half, low_half = slice(0, 64), slice(64, 128)
+
+    def y_first(q):
+        at = 6 * q
+        product(q)
+        stage(at, GW[q, yo, top_half])
+        stage(at + 1, GW[q, yo, low_half])
+        stage(at + 4, GW[q, yr, low_half])
+        pass_on(at, to_right)
+        pass_on(at + 1, to_left)
+        stage(at + 5, GW[q, yl, top_half])
+        pass_on(at + 4, to_right)
+        pass_on(at + 5, to_left)
+
+    def y_second(q):
+        at = 6 * q
+        take(YR.at[at], ysem.at[at])
+        stage(at + 2, GW[q, yr, top_half] + YR[at].astype(F32))
+        take(YR.at[at + 1], ysem.at[at + 1])
+        stage(at + 3, GW[q, yl, low_half] + YR[at + 1].astype(F32))
+        pass_on(at + 2, to_right)
+        pass_on(at + 3, to_left)
+
+    def y_third(q):
+        at = 6 * q
+        for part, one, two in ((top_half, at + 2, at + 5), (low_half, at + 3, at + 4)):
             take(YR.at[two], ysem.at[two])
             take(YR.at[one], ysem.at[one])
-            value = GW[p, y] + YR[one].astype(F32) + YR[two].astype(F32)
-            gw_out[pl.ds(p * 128, 128), :] = value.astype(BF16)
-
-    lax.fori_loop(0, NZ, step, 0)
-    y_first(0)
-    lax.fori_loop(NZ, NZ + 1, step, 0)
-    y_second(0)
-
-    take(STB.at[pl.ds(0, NX - 1)], ssem.at[3])
-    top, total, found = merge(STB, NX)
-    logprob = found - (top + jnp.log(total))
-    lp_out[...] = logprob
-    weight = jnp.where(lane.astype(F32) < LSC[k], WSC[k], 0.0)
-    LZ[k] = jnp.broadcast_to(-jnp.sum(weight * logprob, axis=1, keepdims=True), (1, 128))
-
-    lax.fori_loop(NZ + 1, NZ + SKEW, step, 0)
-    for i in range(1, NZ):
-        put(LZ.at[k], LZ.at[k], sends.at[10], ssem.at[4], {"zl": lax.rem(k + i, NZ)})
-    y_first(1)
-    partial(k)
-    y_third(0)
+            value = GW[q, y, part] + YR[one].astype(F32) + YR[two].astype(F32)
+            gw_out[pl.ds(q * 128 + part.start, 64), :] = value.astype(BF16)
+
+    def finish_stats():
+        take(STB.at[pl.ds(0, NX - 1)], ssem.at[3])
+        top, total, found = merge(STB, NX)
+        logprob = found - (top + jnp.log(total))
+        lp_out[...] = logprob
+        weight = jnp.where(lane.astype(F32) < LSC[k], WSC[k], 0.0)
+        LZ[k] = jnp.broadcast_to(-jnp.sum(weight * logprob, axis=1, keepdims=True), (1, 128))
+
+    def loss_over_z():
+        for i in range(1, NZ):
+            put(LZ.at[k], LZ.at[k], sends.at[10], ssem.at[4], {"zl": lax.rem(k + i, NZ)})
+
+    def loss_over_y():
+        take(LZ.at[pl.ds(0, NZ - 1)], ssem.at[4])
+        LY[y] = jnp.sum(LZ[...], axis=0)
+        for i in range(1, NY):
+            put(LY.at[y], LY.at[y], sends.at[12], ssem.at[5], {"y": lax.rem(y + i, NY)})
 
     def add_side(side):
         for q in range(SUB):
@@ -420,16 +430,30 @@
             take(RB.at[side, k, part], rsem.at[side, k, q])
         PF[k] = PF[k] + RB[side, k].astype(F32)
 
-    pl.when(k > 0)(lambda: add_side(0))
-    pl.when(k < NZ - 1)(lambda: add_side(1))
-    gmix_out[...] = PF[k].astype(BF16)
-
-    y_second(1)
-    take(LZ.at[pl.ds(0, NZ - 1)], ssem.at[4])
-    LY[y] = jnp.sum(LZ[...], axis=0)
-    for i in range(1, NY):
-        put(LY.at[y], LY.at[y], sends.at[12], ssem.at[5], {"y": lax.rem(y + i, NY)})
-    y_third(1)
+    def close_mix():
+        partial(k)
+        pl.when(k > 0)(lambda: add_side(0))
+        pl.when(k < NZ - 1)(lambda: add_side(1))
+        gmix_out[...] = PF[k].astype(BF16)
+
+    ready = (NZ - 1 + OFF, NZ - 1 + OFF + SKEW)
+    last = max(LAG + NZ - 2, ready[1])
+    early, late = range(CUT), range(CUT, SUB)
+    plan = [(JOIN_AT + 2, finish_stats), (JOIN_AT + 2, loss_over_z), (last - 1, loss_over_y)]
+    plan += [(ready[0], lambda q=q: y_first(q)) for q in early]
+    plan += [(ready[1], lambda q=q: y_first(q)) for q in late]
+    plan += [(ready[0] + 1, lambda q=q: y_second(q)) for q in early]
+    plan += [(last, close_mix)]
+    plan += [(ready[1] + 1, lambda q=q: y_second(q)) for q in late]
+    plan += [(ready[0] + 2, lambda q=q: y_third(q)) for q in early]
+    plan += [(ready[1] + 2, lambda q=q: y_third(q)) for q in late]
+    at = 0
+    for turn in sorted({min(when, last) for when, _ in plan}):
+        lax.fori_loop(at, turn + 1, step, 0)
+        at = turn + 1
+        for when, act in plan:
+            if min(when, last) == turn:
+                act()
     take(LY.at[pl.ds(0, NY - 1)], ssem.at[5])
     loss_out[...] = jnp.sum(LY[...], axis=0)
 
@@ -492,8 +516,8 @@
             pltpu.VMEM((2, NZ, rows, heads), BF16),
             pltpu.VMEM((NZ, rows, heads), BF16),
             pltpu.VMEM((SUB, NY, heads // SUB, depth), F32),
-            pltpu.VMEM((12, heads // SUB, depth), BF16),
-            pltpu.VMEM((12, heads // SUB, depth), BF16),
+            pltpu.VMEM((6 * SUB, heads // SUB // 2, depth), BF16),
+            pltpu.VMEM((6 * SUB, heads // SUB // 2, depth), BF16),
             pltpu.VMEM((NY * NZ, 1, 128), F32),
             pltpu.VMEM((NY * NZ, 1, 128), F32),
             pltpu.VMEM((NY * NZ, 1, 128), F32),
@@ -504,7 +528,7 @@
             pltpu.VMEM((NZ, 1, 128), F32),
             pltpu.VMEM((NY, 1, 128), F32),
             dma((4,)), dma((NZ,)), dma((4, NZ)), dma((NZ,)), dma((NZ, SUB)), dma((6,)),
-            dma((2, NZ, SUB)), dma((12,)), dma((6,)), dma((2, NZ)), dma((13,)),
+            dma((2, NZ, SUB)), dma((6 * SUB,)), dma((6,)), dma((2, NZ)), dma((13,)),
         ],
         compiler_params=pltpu.CompilerParams(
             collective_id=0, has_side_effects=True, vmem_limit_bytes=58 * 1024 * 1024

time: 76.6 us -> 71.1 us (0.928)
  the two profiles are of different devices: /device:TPU:4 before, /device:TPU:32 now
where the time goes in v4:
time: 71.1 us; the launch traced here: 71 us
  Pallas kernels  69 us (97%)
  between operations  1.93 us (3%)
    pallas_call x1, Pallas kernels, shards(): pl.pallas_call(kernel, name='step', out_shape=(jax.ShapeDtypeStruct((1, r...  67.2 us
    pallas_call x1, Pallas kernels, shards(): pl.pallas_call(finish, name='finish', out_shape=(jax.ShapeDtypeStruct((1,...  1.8 us

profile of v4, /device:TPU:32, one launch (start us, length us, event | category | flops | bytes accessed | tf_op | source)
XLA Modules:
  0.0 71.0 jit_solution(5946093840727861869)
XLA Ops:
  1.9 67.2 %step.1 = (f32[1,128]{1,0:T(1,128)}, f32[1,128]{1,0:T(1,128)}, bf16[128,512]{1,0:T(8,128)(2,1)}, bf16[512,256]{1,0:T(8,128)(2,1)}) custom-call(bf16[128,4096]{1,0:T(8,128)(2,1)} %logits.1, s32[1,128]{1,0:T(1,128)} %bitcast.8, s32[1,128]{1,0:T(1,128)} %bitcast.9, s32[1,1]{1,0:T(1,128)} %bitcast.6.rewards, s32[1,1]{1,0:T(1,128)} %bitcast.7.groups, ...), custom_call_target="tpu_custom_call" | custom-call | tf_op jit(solution)/shard_map/step/pallas_call | solution.py:496
  69.2 1.8 %finish.1 = (f32[1,128]{1,0:T(1,128)}, f32[1,1]{1,0:T(1,128)}, bf16[128,512]{1,0:T(8,128)(2,1)}, bf16[512,256]{1,0:T(8,128)(2,1)}) custom-call(f32[1,128]{1,0:T(1,128)} %get-tuple-element.12.lp, f32[1,128]{1,0:T(1,128)} %get-tuple-element.13.loss, bf16[128,512]{1,0:T(8,128)(2,1)} %get-tuple-element.14.gmix, bf16[512,256]{1,0:T(8,128)(2,1)} %get-tuple-element.15.gw), custom_call_target="tpu_custom_call" | custom-call | tf_op jit(solution)/shard_map/finish/pallas_call | solution.py:541
